TPU v7x, 32 devices: a whole 2x2x4 slice. The times are simulated.
32 devices in a mesh: ep: 4 (over z), fsdp: 8 (over y, x, core).
Axes of the slice: x: 2, y: 2, z: 4, core: 2. Of those that a mesh axis runs over, the one named last changes fastest.
Arguments:
- train_gate: float32 [64, 2048, 1408], P('ep', 'fsdp'), may hold values from -0.1875 to 0.1875
- train_up: float32 [64, 2048, 1408], P('ep', 'fsdp'), may hold values from -0.1875 to 0.1875
- train_down: float32 [64, 1408, 2048], P('ep', None, 'fsdp'), may hold values from -0.21875 to 0.21875
- router_weight: float32 [2048, 64], P('fsdp', 'ep'), may hold values from -0.125 to 0.125
- router_gain: float32 [2048], P('fsdp'), may hold values from 0.25 to 1.75
Outputs:
- ready_gate: bfloat16 [64, 2048, 1408], P('ep', None, 'fsdp')
- ready_up: bfloat16 [64, 2048, 1408], P('ep', None, 'fsdp')
- ready_down: bfloat16 [64, 1408, 2048], P('ep', 'fsdp')
- scale_gate: float32 [64, 1408], P('ep', 'fsdp')
- scale_up: float32 [64, 1408], P('ep', 'fsdp')
- scale_down: float32 [64, 1408], P('ep', 'fsdp')
- serve_router: bfloat16 [2048, 64], replicated
All inputs are finite; a program needn't handle non-finite values. Where the computation divides by a largest or mean magnitude, that divisor is 1e-20 or more.
Results may differ from a plain program's by a relative error of at most 0.012.
Values may be sent and summed in bfloat16 or wider, within the bound.
A program may use at most 192 MiB of HBM per device.

v0:
```python
import jax
import jax.numpy as jnp
from jax import lax
from jax.sharding import PartitionSpec as P

D_MODEL = 2048


def shards(train_gate, train_up, train_down, router_weight, router_gain):
    total_gate, total_up, total_down = (
        lax.psum(jnp.sum(jnp.abs(train_gate), axis=1).astype(jnp.bfloat16), "fsdp").astype(
            jnp.float32
        ),
        lax.psum(jnp.sum(jnp.abs(train_up), axis=1).astype(jnp.bfloat16), "fsdp").astype(
            jnp.float32
        ),
        lax.psum(jnp.sum(jnp.abs(train_down), axis=2).astype(jnp.bfloat16), "fsdp").astype(
            jnp.float32
        ),
    )
    scale_gate = total_gate / D_MODEL
    scale_up = total_up / D_MODEL
    scale_down = total_down / D_MODEL
    narrow_gate, narrow_up, narrow_down = (
        (train_gate / jnp.expand_dims(scale_gate, 1)).astype(jnp.bfloat16),
        (train_up / jnp.expand_dims(scale_up, 1)).astype(jnp.bfloat16),
        (train_down / jnp.expand_dims(scale_down, 2)).astype(jnp.bfloat16),
    )
    ready_gate, ready_up = (
        lax.all_to_all(narrow_gate, "fsdp", split_axis=2, concat_axis=1, tiled=True),
        lax.all_to_all(narrow_up, "fsdp", split_axis=2, concat_axis=1, tiled=True),
    )
    ready_down = lax.all_to_all(narrow_down, "fsdp", split_axis=1, concat_axis=2, tiled=True)
    scale_gate = lax.dynamic_slice_in_dim(
        scale_gate, lax.axis_index("fsdp") * ready_gate.shape[2], ready_gate.shape[2], axis=1
    )
    scale_up = lax.dynamic_slice_in_dim(
        scale_up, lax.axis_index("fsdp") * ready_up.shape[2], ready_up.shape[2], axis=1
    )
    scale_down = lax.dynamic_slice_in_dim(
        scale_down, lax.axis_index("fsdp") * ready_down.shape[1], ready_down.shape[1], axis=1
    )
    part_router = (router_weight * router_gain[:, None]).astype(jnp.bfloat16)
    row_router = lax.all_gather(part_router, "fsdp", axis=0, tiled=True)
    serve_router = lax.all_gather(row_router, "ep", axis=1, tiled=True)
    return (ready_gate, ready_up, ready_down, scale_gate, scale_up, scale_down, serve_router)


def solution(mesh):
    in_specs = (
        P("ep", "fsdp", None),
        P("ep", "fsdp", None),
        P("ep", None, "fsdp"),
        P("fsdp", "ep"),
        P("fsdp"),
    )
    out_specs = (
        P("ep", None, "fsdp"),
        P("ep", None, "fsdp"),
        P("ep", "fsdp", None),
        P("ep", "fsdp"),
        P("ep", "fsdp"),
        P("ep", "fsdp"),
        P(),
    )
    return jax.shard_map(shards, mesh=mesh, in_specs=in_specs, out_specs=out_specs, check_vma=False)
```

profile of v0, /device:TPU:0, one launch (start us, length us, event | category | flops | bytes accessed | tf_op | source)
XLA Modules:
  0.0 617.4 jit_solution(11987987628351158617)
XLA Ops:
  7.2 0.0 all-reduce.3.cloned.1.call-start
  7.2 0.0 copy-start
  7.2 9.2 %abs_reduce_fusion = bf16[16,1408]{1,0:T(8,128)(2,1)} fusion(f32[16,1408,256]{2,1,0:T(8,128)} %param.7), kind=kLoop, calls=%fused_computation.2 | loop fusion | flops 11511808 | bytes 23113728 | tf_op jit(solution)/shard_map/reduce_sum | solution.py:17
  16.4 5.0 copy-done
  21.4 11.7 %abs_reduce_fusion.1 = (bf16[16,1408]{1,0:T(8,128)(2,1)}, bf16[16,1408]{1,0:T(8,128)(2,1)}) fusion(f32[16,256,1408]{2,1,0:T(8,128)S(1)} %copy-done, f32[16,256,1408]{2,1,0:T(8,128)} %param.5), kind=kLoop, calls=%fused_computation.4 | loop fusion | flops 23023616 | bytes 46227456 | tf_op jit(solution)/shard_map/reduce_sum | solution.py:14
  33.1 0.0 all-reduce.3.cloned.1.call-update
  33.1 23.7 %copy.28 = f32[16,256,1408]{1,0,2:T(8,128)} copy(f32[16,256,1408]{2,1,0:T(8,128)} %param.6) | data formatting | bytes 46137344 | tf_op args[1]
  56.8 31.4 %all-reduce.3.cloned.1.call-done = (bf16[16,1408]{1,0:T(8,128)(2,1)}, bf16[16,1408]{1,0:T(8,128)(2,1)}, bf16[16,1408]{1,0:T(8,128)(2,1)}) async-done(((bf16[16,1408]{1,0:T(8,128)(2,1)}, bf16[16,1408]{1,0:T(8,128)(2,1)}, bf16[16,1408]{1,0:T(8,128)(2,1)}), (bf16[16,1408]{1,0:T(8,128)(2,1)}, bf16[16,1408]{1,0:T(8,128)(2,1)}, bf16[16,1408]{1,0:T(8,128)(2,1)})) %all-reduce.3.cloned.1.call-update) | async-done | bytes 135184 | tf_op jit(solution)/shard_map/psum | solution.py:11
  88.3 0.8 convert_multiply_fusion.1
  89.1 0.3 copy.27
  89.3 14.2 %divide_convert_fusion = bf16[16,256,1408]{1,0,2:T(8,128)(2,1)} fusion(f32[16,256,1408]{1,0,2:T(8,128)} %copy.28, f32[16,1408]{0,1:T(8,128)S(1)} %copy.27), kind=kLoop, calls=%fused_computation.3 | loop fusion | flops 11534336 | bytes 34693120 | tf_op jit(solution)/shard_map/convert_element_type | solution.py:26
  103.5 5.2 all-to-all-start.1
  108.8 0.0 copy-start.2
  108.8 23.7 %copy.24 = f32[16,256,1408]{1,0,2:T(8,128)} copy(f32[16,256,1408]{2,1,0:T(8,128)} %param.5) | data formatting | bytes 46137344 | tf_op args[0]
  132.5 0.0 copy-done.2
  132.5 0.3 copy.23
  132.8 0.0 copy-start.1
  132.8 14.2 %divide_convert_fusion.1 = bf16[16,256,1408]{1,0,2:T(8,128)(2,1)} fusion(f32[16,256,1408]{1,0,2:T(8,128)} %copy.24, f32[16,1408]{0,1:T(8,128)S(1)} %copy.23), kind=kLoop, calls=%fused_computation.5 | loop fusion | flops 11534336 | bytes 34693120 | tf_op jit(solution)/shard_map/convert_element_type | solution.py:25
  147.0 89.5 %all-to-all-done.1 = bf16[16,256,1408]{1,0,2:T(8,128)(2,1)} async-done(((bf16[16,256,1408]{1,0,2:T(8,128)(2,1)}), bf16[16,256,1408]{1,0,2:T(8,128)(2,1)}, u32[]{:S(2)}, u32[]{:S(2)}) %all-to-all-start.1) | async-done | bytes 11534368 | tf_op jit(solution)/shard_map/all_to_all | solution.py:31
  236.5 5.3 all-to-all-start
  241.8 0.0 copy-done.1
  241.8 0.3 copy.31
  242.1 0.0 copy-start.3
  242.1 0.0 copy-start.4
  242.1 32.6 %fusion = bf16[16,1408,256]{2,0,1:T(8,128)(2,1)} fusion(f32[16,1408,256]{2,1,0:T(8,128)} %param.7, f32[16,1408]{0,1:T(8,128)S(1)} %copy.31), kind=kLoop, calls=%fused_computation.1 | loop fusion | flops 11534336 | bytes 34693120 | tf_op jit(solution)/shard_map/convert_element_type | solution.py:27
  274.7 94.8 %all-to-all-done = bf16[16,256,1408]{1,0,2:T(8,128)(2,1)} async-done(((bf16[16,256,1408]{1,0,2:T(8,128)(2,1)}), bf16[16,256,1408]{1,0,2:T(8,128)(2,1)}, u32[]{:S(2)}, u32[]{:S(2)}) %all-to-all-start) | async-done | bytes 11534368 | tf_op jit(solution)/shard_map/all_to_all | solution.py:30
  369.6 5.3 all-to-all-start.2
  374.8 0.0 copy-done.3
  374.8 0.0 copy-done.4
  374.9 130.9 %all_gather.6 = bf16[2048,16]{0,1:T(8,128)(2,1)S(1)} all-gather(bf16[256,16]{0,1:T(8,128)(2,1)S(1)} %multiply_convert_fusion), channel_id=1, replica_groups=mesh['ep'=4,'fsdp'=8] {'fsdp'}, dimensions={0}, use_global_device_ids=true | all-gather | bytes 73728 | tf_op jit(solution)/shard_map/all_gather | solution.py:44
  505.8 14.2 %all_gather.7 = bf16[2048,64]{0,1:T(8,128)(2,1)S(1)} all-gather(bf16[2048,16]{0,1:T(8,128)(2,1)S(1)} %all_gather.6), channel_id=1, replica_groups=mesh['ep'=4,'fsdp'=8] {'ep'}, dimensions={1}, use_global_device_ids=true | all-gather | bytes 327680 | tf_op jit(solution)/shard_map/all_gather | solution.py:45
  519.9 0.7 constant_dynamic-slice_fusion
  520.6 0.7 constant_dynamic-slice_fusion.1
  521.3 0.7 constant_dynamic-slice_fusion.2
  522.0 11.3 %copy.30 = bf16[16,8,256,176]{2,1,3,0:T(8,128)(2,1)} copy(bf16[16,8,256,176]{2,0,3,1:T(8,128)(2,1)} %bitcast.5) | data formatting | bytes 23068672 | tf_op jit(solution)/shard_map/all_to_all | solution.py:31
  533.3 18.0 %all_to_all.46 = bf16[16,2048,176]{1,2,0:T(8,128)(2,1)} reshape(bf16[16,8,256,176]{2,1,3,0:T(8,128)(2,1)} %copy.30) | data formatting | bytes 23068672 | tf_op jit(solution)/shard_map/all_to_all | solution.py:31
  551.3 11.3 %copy.26 = bf16[16,8,256,176]{2,1,3,0:T(8,128)(2,1)} copy(bf16[16,8,256,176]{2,0,3,1:T(8,128)(2,1)} %bitcast.2) | data formatting | bytes 23068672 | tf_op jit(solution)/shard_map/all_to_all | solution.py:30
  562.6 18.0 %all_to_all.42 = bf16[16,2048,176]{1,2,0:T(8,128)(2,1)} reshape(bf16[16,8,256,176]{2,1,3,0:T(8,128)(2,1)} %copy.26) | data formatting | bytes 23068672 | tf_op jit(solution)/shard_map/all_to_all | solution.py:30
  580.6 0.0 all-to-all-done.2
  580.6 11.3 %copy.33 = bf16[16,176,8,256]{3,2,1,0:T(8,128)(2,1)} copy(bf16[16,176,8,256]{3,0,1,2:T(8,128)(2,1)} %bitcast.7) | data formatting | bytes 23068672 | tf_op jit(solution)/shard_map/all_to_all | solution.py:33
  591.9 18.0 %all_to_all.50 = bf16[16,176,2048]{2,1,0:T(8,128)(2,1)} reshape(bf16[16,176,8,256]{3,2,1,0:T(8,128)(2,1)} %copy.33) | data formatting | bytes 23068672 | tf_op jit(solution)/shard_map/all_to_all | solution.py:33
  609.9 0.7 copy.43
  (3 shorter events, 0.0 us)
Async XLA Ops:
  7.2 81.1 %all-reduce.3.cloned.1.call-start = ((), (), s32[]{:S(2)}) async-start(), calls=%async_computation.3 | async-start | bytes 270336 | tf_op jit(solution)/shard_map/psum | solution.py:11
  7.2 14.2 %copy-start = (f32[16,256,1408]{2,1,0:T(8,128)S(1)}, f32[16,256,1408]{2,1,0:T(8,128)}, u32[]{:S(2)}) copy-start(f32[16,256,1408]{2,1,0:T(8,128)} %param.6) | copy-start | bytes 69206016
  103.5 133.0 %all-to-all-start.1 = ((bf16[16,256,1408]{1,0,2:T(8,128)(2,1)}), bf16[16,256,1408]{1,0,2:T(8,128)(2,1)}, u32[]{:S(2)}, u32[]{:S(2)}) async-start(bf16[16,256,1408]{1,0,2:T(8,128)(2,1)} %divide_convert_fusion), calls=%async_computation.1 | async-start | bytes 23068672 | tf_op jit(solution)/shard_map/all_to_all | solution.py:31
  108.8 23.7 %copy-start.2 = (bf16[16,1408]{1,0:T(8,128)(2,1)S(1)}, bf16[16,1408]{1,0:T(8,128)(2,1)}, u32[]{:S(2)}) copy-start(bf16[16,1408]{1,0:T(8,128)(2,1)} %get-tuple-element.7) | copy-start | bytes 135172
  132.8 109.0 %copy-start.1 = (bf16[16,1408]{1,0:T(8,128)(2,1)S(1)}, bf16[16,1408]{1,0:T(8,128)(2,1)}, u32[]{:S(2)}) copy-start(bf16[16,1408]{1,0:T(8,128)(2,1)} %get-tuple-element.9) | copy-start | bytes 135172
  236.5 133.0 %all-to-all-start = ((bf16[16,256,1408]{1,0,2:T(8,128)(2,1)}), bf16[16,256,1408]{1,0,2:T(8,128)(2,1)}, u32[]{:S(2)}, u32[]{:S(2)}) async-start(bf16[16,256,1408]{1,0,2:T(8,128)(2,1)} %divide_convert_fusion.1), calls=%async_computation | async-start | bytes 23068672 | tf_op jit(solution)/shard_map/all_to_all | solution.py:30
  242.1 132.7 %copy-start.3 = (f32[256,16]{0,1:T(8,128)S(1)}, f32[256,16]{0,1:T(8,128)}, u32[]{:S(2)}) copy-start(f32[256,16]{0,1:T(8,128)} %param.8) | copy-start | bytes 49156
  242.1 132.7 %copy-start.4 = (f32[256]{0:T(256)S(1)}, f32[256]{0:T(256)}, u32[]{:S(2)}) copy-start(f32[256]{0:T(256)} %param.9) | copy-start | bytes 3076
  369.6 211.0 %all-to-all-start.2 = ((bf16[16,1408,256]{2,0,1:T(8,128)(2,1)}), bf16[16,1408,256]{2,0,1:T(8,128)(2,1)}, u32[]{:S(2)}, u32[]{:S(2)}) async-start(bf16[16,1408,256]{2,0,1:T(8,128)(2,1)} %fusion), calls=%async_computation.2 | async-start | bytes 23068672 | tf_op jit(solution)/shard_map/all_to_all | solution.py:33
Sparse Core Ops, SparseCore 0:
  33.2 54.9 all-reduce.2
where the time goes:
time: 620 us; the launch traced here: 617 us
  waiting for transfers between devices  216 us (35%)
  blocking collectives  145 us (23%)
  local copies, waits for them, and re-layouts  144 us (23%)
  other arithmetic  82.7 us (13%)
  starting transfers between devices  15.8 us (3%)
  between operations  14.2 us (2%)
    all_gather x1, blocking collectives, shards(): row_router = lax.all_gather(part_router, 'fsdp', axis=0, tiled=True)  131 us
    all_to_all x1, waiting for transfers between devices, shards(): lax.all_to_all(narrow_gate, 'fsdp', split_axis=2, concat_axis=1, tiled=True)  94.8 us
    all_to_all x1, waiting for transfers between devices, shards(): lax.all_to_all(narrow_up, 'fsdp', split_axis=2, concat_axis=1, tiled=True)  89.5 us
    unnamed x13, local copies, waits for them, and re-layouts  53.1 us
    convert_element_type x1, other arithmetic, shards(): (train_down / jnp.expand_dims(scale_down, 2)).astype(jnp.bfloat16)  32.6 us
    psum x1, waiting for transfers between devices, shards(): lax.psum(jnp.sum(jnp.abs(train_gate), axis=1).astype(jnp.bfloat16), 'fsdp')  31.4 us
    all_to_all x2, local copies, waits for them, and re-layouts, shards(): lax.all_to_all(narrow_up, 'fsdp', split_axis=2, concat_axis=1, tiled=True)  29.3 us
    all_to_all x2, local copies, waits for them, and re-layouts, shards(): lax.all_to_all(narrow_gate, 'fsdp', split_axis=2, concat_axis=1, tiled=True)  29.3 us
  transfers between devices with their start and end apart: 4, of which 3 were waited for; matrix products, arithmetic and copies ran while one was open for 19% of the time, Pallas kernels for 0%

commit v1 on v0

v1 whole, which is shorter than its diff:
```python
import functools

import jax
import jax.numpy as jnp
from jax import lax
from jax.experimental import pallas as pl
from jax.experimental.pallas import tpu as pltpu
from jax.sharding import PartitionSpec as P

VMEM_LIMIT = 60 * 1024 * 1024


def pack_kernel(turn, x_ref, *refs):
    out_ref = refs[-1]
    block = x_ref[0]
    if turn:
        block = block.T
    out_ref[...] = block.reshape(out_ref.shape).astype(jnp.bfloat16)


def pack(train, turn, first, count, carried, at, slots, peers):
    _, rows, columns = train.shape
    outer, inner = (columns, rows) if turn else (rows, columns)
    share = outer // peers
    hbm = pl.BlockSpec(memory_space=pl.ANY)
    return pl.pallas_call(
        functools.partial(pack_kernel, turn),
        grid=(count,),
        in_specs=[pl.BlockSpec((1, rows, columns), lambda e: (first + e, 0, 0))] + [hbm] * len(carried),
        out_specs=pl.BlockSpec((peers, 1, share, inner), lambda e: (0, at + e, 0, 0)),
        out_shape=jax.ShapeDtypeStruct((peers, slots, share, inner), jnp.bfloat16),
        input_output_aliases={1: 0} if carried else {},
        compiler_params=pltpu.CompilerParams(vmem_limit_bytes=VMEM_LIMIT),
        cost_estimate=pl.CostEstimate(
            flops=count * rows * columns, bytes_accessed=count * rows * columns * 6, transcendentals=0
        ),
    )(train, *carried)


def finish_kernel(width, x_ref, *refs):
    ready_ref, scale_ref = refs[-2:]
    peers, _, share, inner = x_ref.shape
    total = jnp.zeros((share, inner), jnp.float32)
    for p in range(peers):
        total += jnp.abs(x_ref[p, 0].astype(jnp.float32))
    scale = jnp.sum(total, axis=1, keepdims=True) / width
    for p in range(peers):
        ready_ref[0, :, p * inner : (p + 1) * inner] = (
            x_ref[p, 0].astype(jnp.float32) / scale
        ).astype(jnp.bfloat16)
    scale_ref[0] = jnp.broadcast_to(scale, (share, 128)).T[0:1]


def finish(received, at, count, carried, first, experts):
    peers, _, share, inner = received.shape
    width = peers * inner
    hbm = pl.BlockSpec(memory_space=pl.ANY)
    return pl.pallas_call(
        functools.partial(finish_kernel, width),
        grid=(count,),
        in_specs=[pl.BlockSpec((peers, 1, share, inner), lambda e: (0, at + e, 0, 0))] + [hbm] * len(carried),
        out_specs=[
            pl.BlockSpec((1, share, width), lambda e: (first + e, 0, 0)),
            pl.BlockSpec((1, 1, share), lambda e: (first + e, 0, 0)),
        ],
        out_shape=[
            jax.ShapeDtypeStruct((experts, share, width), jnp.bfloat16),
            jax.ShapeDtypeStruct((experts, 1, share), jnp.float32),
        ],
        input_output_aliases={1: 0, 2: 1} if carried else {},
        compiler_params=pltpu.CompilerParams(vmem_limit_bytes=VMEM_LIMIT),
        cost_estimate=pl.CostEstimate(
            flops=count * share * width * 4, bytes_accessed=count * share * width * 4, transcendentals=0
        ),
    )(received, *carried)


def shards(ep, fsdp, train_gate, train_up, train_down, router_weight, router_gain):
    experts = train_gate.shape[0]
    part = (router_weight * router_gain[:, None]).astype(jnp.bfloat16).T
    copies = jnp.broadcast_to(part[None], (ep * fsdp,) + part.shape)
    router = lax.all_to_all(copies, ("ep", "fsdp"), split_axis=0, concat_axis=0, tiled=True)

    edge = max(experts * 5 // 16, 1)
    plan = (
        (("down", 0, edge),),
        (("down", edge, experts - edge), ("gate", 0, experts), ("up", 0, experts - edge)),
        (("up", experts - edge, edge),),
    )
    train = {"gate": train_gate, "up": train_up, "down": train_down}
    done = {"gate": (), "up": (), "down": ()}

    def pack_group(group):
        slots, at, packed = sum(count for _, _, count in group), 0, ()
        for name, first, count in group:
            packed = (pack(train[name], name != "down", first, count, packed, at, slots, fsdp),)
            at += count
        return packed[0]

    def finish_group(group, received):
        at = 0
        for name, first, count in group:
            done[name] = finish(received, at, count, done[name], first, experts)
            at += count

    def exchange(packed):
        return lax.all_to_all(packed, "fsdp", split_axis=0, concat_axis=0, tiled=True)

    packed, router = lax.optimization_barrier((pack_group(plan[0]), router))
    received = exchange(packed)
    for last, group in zip(plan, plan[1:]):
        received, packed, done = lax.optimization_barrier((received, pack_group(group), done))
        arrived, received = received, exchange(packed)
        finish_group(last, arrived)
    received, done = lax.optimization_barrier((received, done))
    finish_group(plan[-1], received)

    router = router.reshape((ep, fsdp) + part.shape).transpose(1, 3, 0, 2)
    serve_router = router.reshape(fsdp * part.shape[1], ep * part.shape[0])
    (ready_gate, scale_gate), (ready_up, scale_up), (ready_down, scale_down) = (
        done["gate"],
        done["up"],
        done["down"],
    )
    return (
        jnp.swapaxes(ready_gate, 1, 2),
        jnp.swapaxes(ready_up, 1, 2),
        ready_down,
        scale_gate[:, 0],
        scale_up[:, 0],
        scale_down[:, 0],
        serve_router,
    )


def solution(mesh):
    in_specs = (
        P("ep", "fsdp", None),
        P("ep", "fsdp", None),
        P("ep", None, "fsdp"),
        P("fsdp", "ep"),
        P("fsdp"),
    )
    out_specs = (
        P("ep", None, "fsdp"),
        P("ep", None, "fsdp"),
        P("ep", "fsdp", None),
        P("ep", "fsdp"),
        P("ep", "fsdp"),
        P("ep", "fsdp"),
        P(),
    )
    body = functools.partial(shards, mesh.shape["ep"], mesh.shape["fsdp"])
    return jax.shard_map(body, mesh=mesh, in_specs=in_specs, out_specs=out_specs, check_vma=False)
```

time: 620 us -> 432 us (0.70)
  blocking collectives: 145 us -> 0 us
  local copies, waits for them, and re-layouts: 144 us -> 3.51 us
  Pallas kernels: 0 us -> 110 us
  other arithmetic: 82.7 us -> 0.72 us
  waiting for transfers between devices: 216 us -> 291 us
  between operations: 14.2 us -> 0.68 us
  starting transfers between devices: 15.8 us -> 22.9 us
    all_gather x2 -> x0, blocking collectives: 145 us -> none  [the longest x1 131 us: shards(): row_router = lax.all_gather(part_router, 'fsdp', axis=0, tiled=True)]
    pallas_call x0 -> x10, Pallas kernels: none -> 110 us  [the longest x5 58 us: pack(): pl.pallas_call(functools.partial(pack_kernel, turn), grid=(count,), in_sp...]
    all_to_all x3 -> x4, waiting for transfers between devices: 184 us -> 291 us  [the longest x3 286 us: exchange(): lax.all_to_all(packed, 'fsdp', split_axis=0, concat_axis=0, tiled=True)]
    all_to_all x6 -> x0, local copies, waits for them, and re-layouts: 87.9 us -> none  [the longest x2 29.3 us: shards(): lax.all_to_all(narrow_up, 'fsdp', split_axis=2, concat_axis=1, tiled=True)]
    convert_element_type x4 -> x0, other arithmetic: 61 us -> none  [the longest x1 32.6 us: shards(): (train_down / jnp.expand_dims(scale_down, 2)).astype(jnp.bfloat16)]
    unnamed x13 -> x7, local copies, waits for them, and re-layouts: 53.1 us -> 2.7 us
    psum x1 -> x0, waiting for transfers between devices: 31.4 us -> none  [shards(): lax.psum(jnp.sum(jnp.abs(train_gate), axis=1).astype(jnp.bfloat16), 'fsdp')]
    reduce_sum x2 -> x0, other arithmetic: 20.8 us -> none  [the longest x1 11.7 us: shards(): jnp.sum(jnp.abs(train_up), axis=1).astype(jnp.bfloat16)]
  transfers between devices with their start and end apart: 4 -> 4, of which waited for: 3 -> 3; matrix products, arithmetic and copies ran while one was open for 19% -> 0% of each run, Pallas kernels for 0% -> 24%
where the time goes in v1:
time: 432 us; the launch traced here: 429 us
  waiting for transfers between devices  291 us (67%)
  Pallas kernels  110 us (25%)
  starting transfers between devices  22.9 us (5%)
    all_to_all x3, waiting for transfers between devices, exchange(): lax.all_to_all(packed, 'fsdp', split_axis=0, concat_axis=0, tiled=True)  286 us
    pallas_call x5, Pallas kernels, pack(): pl.pallas_call(functools.partial(pack_kernel, turn), grid=(count,), in_sp...  58 us
    pallas_call x5, Pallas kernels, finish(): pl.pallas_call(functools.partial(finish_kernel, width), grid=(count,), in...  52.4 us
    all_to_all x3, starting transfers between devices, exchange(): lax.all_to_all(packed, 'fsdp', split_axis=0, concat_axis=0, tiled=True)  15.6 us
  transfers between devices with their start and end apart: 4, of which 3 were waited for; matrix products, arithmetic and copies ran while one was open for 0% of the time, Pallas kernels for 24%

profile of v1, /device:TPU:0, one launch (start us, length us, event | category | flops | bytes accessed | tf_op | source)
XLA Modules:
  0.0 428.8 jit_solution(5097164724395214162)
XLA Ops:
  0.6 0.7 fusion
  1.4 0.7 broadcast_in_dim.2
  2.1 7.3 %all-to-all-start = ((bf16[32,16,256]{2,1,0:T(8,128)(2,1)}), bf16[32,16,256]{2,1,0:T(8,128)(2,1)S(1)}, u32[]{:S(2)}, u32[]{:S(2)}) async-start(bf16[32,16,256]{2,1,0:T(8,128)(2,1)} %broadcast_in_dim.2), calls=%async_computation | async-start | bytes 524288 | tf_op jit(solution)/shard_map/all_to_all | solution.py:82
  9.4 6.4 %shard_map.108 = bf16[8,5,176,256]{3,2,1,0:T(8,128)(2,1)} custom-call(f32[16,1408,256]{2,1,0:T(8,128)} %x_ref.6), custom_call_target="tpu_custom_call" | custom-call | flops 1802240 | bytes 10813440 | tf_op jit(solution)/shard_map/pallas_call | solution.py:26
  15.8 4.2 all-to-all-done
  20.0 4.5 %all-to-all-start.1 = ((bf16[8,5,176,256]{3,2,1,0:T(8,128)(2,1)}), bf16[8,5,176,256]{3,2,1,0:T(8,128)(2,1)}, u32[]{:S(2)}, u32[]{:S(2)}) async-start(bf16[8,5,176,256]{3,2,1,0:T(8,128)(2,1)} %shard_map.108), calls=%async_computation.1 | async-start | bytes 7208960 | tf_op jit(solution)/shard_map/all_to_all | solution.py:107
  24.5 12.6 %shard_map.109.refs_0_ = bf16[8,38,176,256]{3,2,1,0:T(8,128)(2,1)} custom-call(f32[16,1408,256]{2,1,0:T(8,128)} %x_ref.6), custom_call_target="tpu_custom_call" | custom-call | flops 3964928 | bytes 23789568 | tf_op jit(solution)/shard_map/pallas_call | solution.py:26
  37.1 18.5 %shard_map.110.refs_0_ = bf16[8,38,176,256]{3,2,1,0:T(8,128)(2,1)} custom-call(f32[16,256,1408]{2,1,0:T(8,128)} %x_ref.7, bf16[8,38,176,256]{3,2,1,0:T(8,128)(2,1)} %shard_map.109.refs_0_), custom_call_target="tpu_custom_call", output_to_operand_aliasing={{}: (1, {})} | custom-call | flops 5767168 | bytes 34603008 | tf_op jit(solution)/shard_map/pallas_call | solution.py:26
  55.6 13.6 %shard_map.111 = bf16[8,38,176,256]{3,2,1,0:T(8,128)(2,1)} custom-call(f32[16,256,1408]{2,1,0:T(8,128)} %x_ref.9, bf16[8,38,176,256]{3,2,1,0:T(8,128)(2,1)} %shard_map.110.refs_0_), custom_call_target="tpu_custom_call", output_to_operand_aliasing={{}: (1, {})} | custom-call | flops 3964928 | bytes 23789568 | tf_op jit(solution)/shard_map/pallas_call | solution.py:26
  69.2 0.0 all-to-all-done.1.x_ref
  69.2 6.6 %all-to-all-start.2 = ((bf16[8,38,176,256]{3,2,1,0:T(8,128)(2,1)}), bf16[8,38,176,256]{3,2,1,0:T(8,128)(2,1)}, u32[]{:S(2)}, u32[]{:S(2)}) async-start(bf16[8,38,176,256]{3,2,1,0:T(8,128)(2,1)} %shard_map.111), calls=%async_computation.2 | async-start | bytes 54788096 | tf_op jit(solution)/shard_map/all_to_all | solution.py:107
  75.8 6.9 %shard_map.112 = bf16[8,5,176,256]{3,2,1,0:T(8,128)(2,1)} custom-call(f32[16,256,1408]{2,1,0:T(8,128)} %x_ref.9), custom_call_target="tpu_custom_call" | custom-call | flops 1802240 | bytes 10813440 | tf_op jit(solution)/shard_map/pallas_call | solution.py:26
  82.7 6.1 %shard_map.113 = (bf16[16,176,2048]{2,1,0:T(8,128)(2,1)}, f32[16,1,176]{2,1,0:T(1,128)}) custom-call(bf16[8,5,176,256]{3,2,1,0:T(8,128)(2,1)} %all-to-all-done.1.x_ref), custom_call_target="tpu_custom_call" | custom-call | flops 7208960 | bytes 7208960 | tf_op jit(solution)/shard_map/pallas_call | solution.py:58
  88.8 284.6 %all-to-all-done.2.x_ref = bf16[8,38,176,256]{3,2,1,0:T(8,128)(2,1)} async-done(((bf16[8,38,176,256]{3,2,1,0:T(8,128)(2,1)}), bf16[8,38,176,256]{3,2,1,0:T(8,128)(2,1)}, u32[]{:S(2)}, u32[]{:S(2)}) %all-to-all-start.2) | async-done | bytes 27394080 | tf_op jit(solution)/shard_map/all_to_all | solution.py:107
  373.4 4.5 %all-to-all-start.3 = ((bf16[8,5,176,256]{3,2,1,0:T(8,128)(2,1)}), bf16[8,5,176,256]{3,2,1,0:T(8,128)(2,1)}, u32[]{:S(2)}, u32[]{:S(2)}) async-start(bf16[8,5,176,256]{3,2,1,0:T(8,128)(2,1)} %shard_map.112), calls=%async_computation.3 | async-start | bytes 7208960 | tf_op jit(solution)/shard_map/all_to_all | solution.py:107
  377.9 0.1 copy.18
  378.0 0.8 copy.22
  378.8 12.0 %shard_map.116 = (bf16[16,176,2048]{2,1,0:T(8,128)(2,1)}, f32[16,1,176]{2,1,0:T(1,128)}) custom-call(bf16[8,38,176,256]{3,2,1,0:T(8,128)(2,1)} %all-to-all-done.2.x_ref), custom_call_target="tpu_custom_call" | custom-call | flops 15859712 | bytes 15859712 | tf_op jit(solution)/shard_map/pallas_call | solution.py:58
  390.7 12.0 %shard_map.114 = (bf16[16,176,2048]{2,1,0:T(8,128)(2,1)}, f32[16,1,176]{2,1,0:T(1,128)}) custom-call(bf16[8,38,176,256]{3,2,1,0:T(8,128)(2,1)} %all-to-all-done.2.x_ref, bf16[16,176,2048]{2,1,0:T(8,128)(2,1)} %get-tuple-element.39.refs_0_, f32[16,1,176]{2,1,0:T(1,128)} %get-tuple-element.40.refs_1_), custom_call_target="tpu_custom_call", output_to_operand_aliasing={{0}: (1, {}), {1}: (2, {})} | custom-call | flops 15859712 | bytes 15859712 | tf_op jit(solution)/shard_map/pallas_call | solution.py:58
  402.7 16.2 %shard_map.115 = (bf16[16,176,2048]{2,1,0:T(8,128)(2,1)}, f32[16,1,176]{2,1,0:T(1,128)}) custom-call(bf16[8,38,176,256]{3,2,1,0:T(8,128)(2,1)} %all-to-all-done.2.x_ref), custom_call_target="tpu_custom_call" | custom-call | flops 23068672 | bytes 23068672 | tf_op jit(solution)/shard_map/pallas_call | solution.py:58
  418.9 0.0 copy-start
  418.9 0.0 copy-start.1
  418.9 1.8 all-to-all-done.3.x_ref
  420.7 6.1 %shard_map.117 = (bf16[16,176,2048]{2,1,0:T(8,128)(2,1)}, f32[16,1,176]{2,1,0:T(1,128)}) custom-call(bf16[8,5,176,256]{3,2,1,0:T(8,128)(2,1)} %all-to-all-done.3.x_ref, bf16[16,176,2048]{2,1,0:T(8,128)(2,1)} %get-tuple-element.49.refs_0_, f32[16,1,176]{2,1,0:T(1,128)} %get-tuple-element.50.refs_1_), custom_call_target="tpu_custom_call", output_to_operand_aliasing={{0}: (1, {}), {1}: (2, {})} | custom-call | flops 7208960 | bytes 7208960 | tf_op jit(solution)/shard_map/pallas_call | solution.py:58
  426.9 1.3 copy.26
  428.2 0.0 copy-done
  428.2 0.0 copy-done.1
  428.2 0.6 copy_bitcast_fusion
Async XLA Ops:
  2.1 17.9 %all-to-all-start = ((bf16[32,16,256]{2,1,0:T(8,128)(2,1)}), bf16[32,16,256]{2,1,0:T(8,128)(2,1)S(1)}, u32[]{:S(2)}, u32[]{:S(2)}) async-start(bf16[32,16,256]{2,1,0:T(8,128)(2,1)} %broadcast_in_dim.2), calls=%async_computation | async-start | bytes 524288 | tf_op jit(solution)/shard_map/all_to_all | solution.py:82
  20.0 49.2 %all-to-all-start.1 = ((bf16[8,5,176,256]{3,2,1,0:T(8,128)(2,1)}), bf16[8,5,176,256]{3,2,1,0:T(8,128)(2,1)}, u32[]{:S(2)}, u32[]{:S(2)}) async-start(bf16[8,5,176,256]{3,2,1,0:T(8,128)(2,1)} %shard_map.108), calls=%async_computation.1 | async-start | bytes 7208960 | tf_op jit(solution)/shard_map/all_to_all | solution.py:107
  69.2 304.3 %all-to-all-start.2 = ((bf16[8,38,176,256]{3,2,1,0:T(8,128)(2,1)}), bf16[8,38,176,256]{3,2,1,0:T(8,128)(2,1)}, u32[]{:S(2)}, u32[]{:S(2)}) async-start(bf16[8,38,176,256]{3,2,1,0:T(8,128)(2,1)} %shard_map.111), calls=%async_computation.2 | async-start | bytes 54788096 | tf_op jit(solution)/shard_map/all_to_all | solution.py:107
  373.4 47.3 %all-to-all-start.3 = ((bf16[8,5,176,256]{3,2,1,0:T(8,128)(2,1)}), bf16[8,5,176,256]{3,2,1,0:T(8,128)(2,1)}, u32[]{:S(2)}, u32[]{:S(2)}) async-start(bf16[8,5,176,256]{3,2,1,0:T(8,128)(2,1)} %shard_map.112), calls=%async_computation.3 | async-start | bytes 7208960 | tf_op jit(solution)/shard_map/all_to_all | solution.py:107
  418.9 9.3 %copy-start = (f32[16,1,176]{2,1,0:T(1,128)S(1)}, f32[16,1,176]{2,1,0:T(1,128)}, u32[]{:S(2)}) copy-start(f32[16,1,176]{2,1,0:T(1,128)} %get-tuple-element.55) | copy-start | bytes 33796
  418.9 9.3 %copy-start.1 = (f32[16,1,176]{2,1,0:T(1,128)S(1)}, f32[16,1,176]{2,1,0:T(1,128)}, u32[]{:S(2)}) copy-start(f32[16,1,176]{2,1,0:T(1,128)} %get-tuple-element.53) | copy-start | bytes 33796
